TPU v7x, 32 devices: a whole 2x2x4 slice. The times are simulated.
32 devices in a mesh: filt: 4 (over y, x), dom: 8 (over z, core).
Axes of the slice: x: 2, y: 2, z: 4, core: 2. Of those that a mesh axis runs over, the one named last changes fastest.
Arguments:
- log_weights: float32 [524288], P(('filt', 'dom')), parts along dimension 0, may hold values from -20 to 250, as said below
- bins: int32 [524288], P(('filt', 'dom')), parts along dimension 0, may hold values from 0 to 4095
- states: bfloat16 [128, 524288], P(None, ('filt', 'dom')), parts along dimension 1, may hold values from -6 to 6
Outputs:
- cumulative: float32 [16384], P(('filt', 'dom')), parts along dimension 0
- bin_means: float32 [128, 16384], P(None, ('filt', 'dom')), parts along dimension 1
- particle_weights: float32 [524288], P(('filt', 'dom')), parts along dimension 0
There are 4 independent parts, one for each index of `filt`. A program takes and returns all parts, laid end to end along the dimension named above; each array names one. Nothing has to cross between parts.
Inputs may be any that keep to these rules, and one draw needn't show every extreme that they name: `log_weights`: finite log-weights.
All inputs are finite; a program needn't handle non-finite values.
Results may differ from a plain program's by a relative error of at most 0.00051.
Values sent between devices are 32-bit elements; how exact they have to be, the bound alone decides.
No kernel may reach another device: no remote copies, remote signals or barrier semaphores. Data moves between devices by JAX's collectives and lax.ppermute only.
A program may use at most 64 MiB of HBM per device.

v0:
```python
import jax
import jax.numpy as jnp
from jax import lax
from jax.sharding import PartitionSpec as P

BINS = 4096


floor_value = -10000.0


def local_pairs(log_weights, bins, states):
    count = log_weights.shape[0]
    width = min(count, 1024)
    blocks = count // width
    labels = lax.iota(jnp.int32, BINS)

    def top_step(index, carry):
        start = index * width
        row_weights = lax.dynamic_slice_in_dim(log_weights, start, width)
        row_bins = lax.dynamic_slice_in_dim(bins, start, width)
        member = row_bins[:, None] == labels[None, :]
        return jnp.maximum(
            carry, jnp.max(jnp.where(member, row_weights[:, None], floor_value), axis=0)
        )

    bin_top = lax.fori_loop(0, blocks, top_step, jnp.full((BINS,), floor_value, jnp.float32))
    ones_row = jnp.ones((1, width), jnp.bfloat16)

    def sum_step(index, carry):
        totals, sums = carry
        start = index * width
        row_weights = lax.dynamic_slice_in_dim(log_weights, start, width)
        row_bins = lax.dynamic_slice_in_dim(bins, start, width)
        row_states = lax.dynamic_slice_in_dim(states, start, width, 1)
        member = row_bins[:, None] == labels[None, :]
        own_top = jnp.take(bin_top, row_bins)
        scaled = jnp.exp(row_weights - own_top).astype(jnp.bfloat16)
        spread = jnp.where(member, scaled[:, None], jnp.zeros((), jnp.bfloat16))
        totals = totals + jnp.dot(ones_row, spread, preferred_element_type=jnp.float32)[0]
        sums = sums + jnp.dot(row_states, spread, preferred_element_type=jnp.float32)
        return (totals, sums)

    start_pair = (jnp.zeros((BINS,), jnp.float32), jnp.zeros((states.shape[0], BINS), jnp.float32))
    totals, sums = lax.fori_loop(0, blocks, sum_step, start_pair)
    return (bin_top, totals, sums)


def body(log_weights, bins, states):
    groups = lax.axis_size("dom")
    owned = BINS // groups
    bin_top, totals, sums = local_pairs(log_weights, bins, states)
    top_pieces, mass_pieces, sum_pieces = (
        lax.all_to_all(bin_top[None, :], "dom", split_axis=1, concat_axis=0, tiled=True),
        lax.all_to_all(totals[None, :], "dom", split_axis=1, concat_axis=0, tiled=True),
        lax.all_to_all(sums, "dom", split_axis=1, concat_axis=0, tiled=True),
    )
    sum_pieces = sum_pieces.reshape(groups, sums.shape[0], owned)
    owned_top = jnp.max(top_pieces, axis=0)
    factor = jnp.exp(top_pieces - owned_top[None, :])
    owned_mass = jnp.sum(mass_pieces * factor, axis=0)
    owned_sums = jnp.sum(sum_pieces * factor[:, None, :], axis=0)
    block_top = jnp.max(owned_top)
    block_mass = jnp.sum(owned_mass * jnp.exp(owned_top - block_top))
    share = None
    all_tops, all_masses = (
        lax.all_gather(block_top[None], "dom", axis=0, tiled=True),
        lax.all_gather(block_mass[None], "dom", axis=0, tiled=True),
    )
    top = jnp.max(all_tops)
    scaled_masses = all_masses * jnp.exp(all_tops - top)
    total = jnp.sum(scaled_masses)
    lower = lax.iota(jnp.int32, groups) < lax.axis_index("dom")
    before = jnp.sum(jnp.where(lower, scaled_masses, jnp.float32(0.0)))
    share = owned_mass * jnp.exp(owned_top - top)
    cumulative = (before + jnp.cumsum(share)) / total
    bin_means = owned_sums / jnp.maximum(owned_mass, 1.0)[None, :]
    whole_count = log_weights.shape[0] * groups
    particle_weights = whole_count * jnp.exp(log_weights - top) / total
    return (cumulative, bin_means, particle_weights)


def solution(mesh):
    placed = (P(("filt", "dom")), P(("filt", "dom")), P(None, ("filt", "dom")))
    return jax.shard_map(
        body,
        mesh=mesh,
        in_specs=placed,
        out_specs=(P(("filt", "dom")), P(None, ("filt", "dom")), P(("filt", "dom"))),
        check_vma=False,
    )
```

profile of v0, /device:TPU:16, one launch (start us, length us, event | category | flops | bytes accessed | tf_op | source)
XLA Modules:
  0.0 426.6 jit_solution(2774227915894027534)
XLA Ops:
  0.7 152.2 %while.30 = (s32[]{:T(128)}, f32[4096]{0:T(1024)}, s32[16384]{0:T(1024)}, f32[16384]{0:T(1024)}, s32[]{:T(128)}, /*index=5*/s32[]{:T(128)}, s32[]{:T(128)}, s32[]{:T(128)}) while((s32[]{:T(128)}, f32[4096]{0:T(1024)}, s32[16384]{0:T(1024)}, f32[16384]{0:T(1024)}, s32[]{:T(128)}, /*index=5*/s32[]{:T(128)}, s32[]{:T(128)}, ...), condition=%wide.region_2.3_spmd.clone, body=%wide.region_0.2_spmd.clone.sunk | while | flops 12587015 | bytes 90269 | solution.py:27
  2.1 6.8 %select_reduce_fusion.2 = f32[4096]{0:T(1024)S(1)} fusion(f32[1024]{0:T(1024)S(1)} %dynamic_slice.49, s32[1024]{0:T(1024)S(1)} %dynamic_slice.50), kind=kLoop, calls=%fused_computation.4.clone.1 | loop fusion | flops 12578816 | bytes 24576 | tf_op jit(solution)/shard_map/while/body/eval_jaxpr/reduce_max | solution.py:24
  10.9 6.8 %select_reduce_fusion.2 = f32[4096]{0:T(1024)S(1)} fusion(f32[1024]{0:T(1024)S(1)} %dynamic_slice.49, s32[1024]{0:T(1024)S(1)} %dynamic_slice.50), kind=kLoop, calls=%fused_computation.4.clone.1 | loop fusion | flops 12578816 | bytes 24576 | tf_op jit(solution)/shard_map/while/body/eval_jaxpr/reduce_max | solution.py:24
  20.4 6.8 %select_reduce_fusion.2 = f32[4096]{0:T(1024)S(1)} fusion(f32[1024]{0:T(1024)S(1)} %dynamic_slice.49, s32[1024]{0:T(1024)S(1)} %dynamic_slice.50), kind=kLoop, calls=%fused_computation.4.clone.1 | loop fusion | flops 12578816 | bytes 24576 | tf_op jit(solution)/shard_map/while/body/eval_jaxpr/reduce_max | solution.py:24
  30.0 6.8 %select_reduce_fusion.2 = f32[4096]{0:T(1024)S(1)} fusion(f32[1024]{0:T(1024)S(1)} %dynamic_slice.49, s32[1024]{0:T(1024)S(1)} %dynamic_slice.50), kind=kLoop, calls=%fused_computation.4.clone.1 | loop fusion | flops 12578816 | bytes 24576 | tf_op jit(solution)/shard_map/while/body/eval_jaxpr/reduce_max | solution.py:24
  39.6 6.8 %select_reduce_fusion.2 = f32[4096]{0:T(1024)S(1)} fusion(f32[1024]{0:T(1024)S(1)} %dynamic_slice.49, s32[1024]{0:T(1024)S(1)} %dynamic_slice.50), kind=kLoop, calls=%fused_computation.4.clone.1 | loop fusion | flops 12578816 | bytes 24576 | tf_op jit(solution)/shard_map/while/body/eval_jaxpr/reduce_max | solution.py:24
  49.1 6.8 %select_reduce_fusion.2 = f32[4096]{0:T(1024)S(1)} fusion(f32[1024]{0:T(1024)S(1)} %dynamic_slice.49, s32[1024]{0:T(1024)S(1)} %dynamic_slice.50), kind=kLoop, calls=%fused_computation.4.clone.1 | loop fusion | flops 12578816 | bytes 24576 | tf_op jit(solution)/shard_map/while/body/eval_jaxpr/reduce_max | solution.py:24
  58.7 6.8 %select_reduce_fusion.2 = f32[4096]{0:T(1024)S(1)} fusion(f32[1024]{0:T(1024)S(1)} %dynamic_slice.49, s32[1024]{0:T(1024)S(1)} %dynamic_slice.50), kind=kLoop, calls=%fused_computation.4.clone.1 | loop fusion | flops 12578816 | bytes 24576 | tf_op jit(solution)/shard_map/while/body/eval_jaxpr/reduce_max | solution.py:24
  68.2 6.8 %select_reduce_fusion.2 = f32[4096]{0:T(1024)S(1)} fusion(f32[1024]{0:T(1024)S(1)} %dynamic_slice.49, s32[1024]{0:T(1024)S(1)} %dynamic_slice.50), kind=kLoop, calls=%fused_computation.4.clone.1 | loop fusion | flops 12578816 | bytes 24576 | tf_op jit(solution)/shard_map/while/body/eval_jaxpr/reduce_max | solution.py:24
  77.8 6.8 %select_reduce_fusion.2 = f32[4096]{0:T(1024)S(1)} fusion(f32[1024]{0:T(1024)S(1)} %dynamic_slice.49, s32[1024]{0:T(1024)S(1)} %dynamic_slice.50), kind=kLoop, calls=%fused_computation.4.clone.1 | loop fusion | flops 12578816 | bytes 24576 | tf_op jit(solution)/shard_map/while/body/eval_jaxpr/reduce_max | solution.py:24
  87.3 6.8 %select_reduce_fusion.2 = f32[4096]{0:T(1024)S(1)} fusion(f32[1024]{0:T(1024)S(1)} %dynamic_slice.49, s32[1024]{0:T(1024)S(1)} %dynamic_slice.50), kind=kLoop, calls=%fused_computation.4.clone.1 | loop fusion | flops 12578816 | bytes 24576 | tf_op jit(solution)/shard_map/while/body/eval_jaxpr/reduce_max | solution.py:24
  96.9 6.8 %select_reduce_fusion.2 = f32[4096]{0:T(1024)S(1)} fusion(f32[1024]{0:T(1024)S(1)} %dynamic_slice.49, s32[1024]{0:T(1024)S(1)} %dynamic_slice.50), kind=kLoop, calls=%fused_computation.4.clone.1 | loop fusion | flops 12578816 | bytes 24576 | tf_op jit(solution)/shard_map/while/body/eval_jaxpr/reduce_max | solution.py:24
  106.4 6.8 %select_reduce_fusion.2 = f32[4096]{0:T(1024)S(1)} fusion(f32[1024]{0:T(1024)S(1)} %dynamic_slice.49, s32[1024]{0:T(1024)S(1)} %dynamic_slice.50), kind=kLoop, calls=%fused_computation.4.clone.1 | loop fusion | flops 12578816 | bytes 24576 | tf_op jit(solution)/shard_map/while/body/eval_jaxpr/reduce_max | solution.py:24
  116.0 6.8 %select_reduce_fusion.2 = f32[4096]{0:T(1024)S(1)} fusion(f32[1024]{0:T(1024)S(1)} %dynamic_slice.49, s32[1024]{0:T(1024)S(1)} %dynamic_slice.50), kind=kLoop, calls=%fused_computation.4.clone.1 | loop fusion | flops 12578816 | bytes 24576 | tf_op jit(solution)/shard_map/while/body/eval_jaxpr/reduce_max | solution.py:24
  125.5 6.8 %select_reduce_fusion.2 = f32[4096]{0:T(1024)S(1)} fusion(f32[1024]{0:T(1024)S(1)} %dynamic_slice.49, s32[1024]{0:T(1024)S(1)} %dynamic_slice.50), kind=kLoop, calls=%fused_computation.4.clone.1 | loop fusion | flops 12578816 | bytes 24576 | tf_op jit(solution)/shard_map/while/body/eval_jaxpr/reduce_max | solution.py:24
  135.1 6.8 %select_reduce_fusion.2 = f32[4096]{0:T(1024)S(1)} fusion(f32[1024]{0:T(1024)S(1)} %dynamic_slice.49, s32[1024]{0:T(1024)S(1)} %dynamic_slice.50), kind=kLoop, calls=%fused_computation.4.clone.1 | loop fusion | flops 12578816 | bytes 24576 | tf_op jit(solution)/shard_map/while/body/eval_jaxpr/reduce_max | solution.py:24
  144.6 6.8 %select_reduce_fusion.2 = f32[4096]{0:T(1024)S(1)} fusion(f32[1024]{0:T(1024)S(1)} %dynamic_slice.49, s32[1024]{0:T(1024)S(1)} %dynamic_slice.50), kind=kLoop, calls=%fused_computation.4.clone.1 | loop fusion | flops 12578816 | bytes 24576 | tf_op jit(solution)/shard_map/while/body/eval_jaxpr/reduce_max | solution.py:24
  152.8 189.3 %while.31 = (s32[]{:T(128)}, f32[4096]{0:T(1024)S(1)}, f32[128,4096]{1,0:T(8,128)S(1)}, s32[16384]{0:T(1024)}, f32[16384]{0:T(1024)}, /*index=5*/f32[4096]{0:T(1...) while((s32[]{:T(128)}, f32[4096]{0:T(1024)S(1)}, ...), condition=%wide.region_4.5_spmd.clone, body=%wide.region_3.4_spmd.clone.sunk | while | flops 1099977728 | bytes 4573370 | solution.py:45
  153.5 5.7 %gather_fusion = f32[1024]{0:T(1024)S(1)} fusion(f32[4096]{0:T(1024)} %get-tuple-element.440, s32[1024]{0:T(1024)S(1)} %get-tuple-element.388), kind=kCustom, calls=%fused_computation.clone.clone.1 | custom fusion | bytes 12288 | tf_op jit(solution)/shard_map/while/body/eval_jaxpr/jit(_take)/gather | solution.py:37
  165.3 5.7 %gather_fusion = f32[1024]{0:T(1024)S(1)} fusion(f32[4096]{0:T(1024)} %get-tuple-element.440, s32[1024]{0:T(1024)S(1)} %get-tuple-element.388), kind=kCustom, calls=%fused_computation.clone.clone.1 | custom fusion | bytes 12288 | tf_op jit(solution)/shard_map/while/body/eval_jaxpr/jit(_take)/gather | solution.py:37
  177.2 5.7 %gather_fusion = f32[1024]{0:T(1024)S(1)} fusion(f32[4096]{0:T(1024)} %get-tuple-element.440, s32[1024]{0:T(1024)S(1)} %get-tuple-element.388), kind=kCustom, calls=%fused_computation.clone.clone.1 | custom fusion | bytes 12288 | tf_op jit(solution)/shard_map/while/body/eval_jaxpr/jit(_take)/gather | solution.py:37
  319.2 5.7 %gather_fusion = f32[1024]{0:T(1024)S(1)} fusion(f32[4096]{0:T(1024)} %get-tuple-element.440, s32[1024]{0:T(1024)S(1)} %get-tuple-element.388), kind=kCustom, calls=%fused_computation.clone.clone.1 | custom fusion | bytes 12288 | tf_op jit(solution)/shard_map/while/body/eval_jaxpr/jit(_take)/gather | solution.py:37
  342.1 8.3 %all_to_all.45 = f32[1,8,512]{2,0,1:T(1,128)S(1)} all-to-all(f32[1,8,512]{2,0,1:T(1,128)S(1)} %bitcast.23), channel_id=1, replica_groups=mesh['filt'=4,'dom'=8] {'dom'}, dimensions={1} | all-to-all | bytes 32768 | tf_op jit(solution)/shard_map/all_to_all | solution.py:55
  370.6 48.1 %all-reduce.2 = (f32[8]{0:T(128)S(1)}, f32[8]{0:T(128)S(1)}) all-reduce(f32[8]{0:T(128)S(1)} %dynamic-update-slice.1, f32[8]{0:T(128)S(1)} %dynamic-update-slice), channel_id=1, replica_groups=mesh['filt'=4,'dom'=8] {'dom'}, use_global_device_ids=true, to_apply=%add.1 | all-reduce | flops 16 | bytes 128
  (174 shorter events, 236.4 us)
Async XLA Ops:
  342.1 13.9 %copy-start = (f32[128,4096]{1,0:T(8,128)}, f32[128,4096]{1,0:T(8,128)S(1)}, u32[]{:S(2)}) copy-start(f32[128,4096]{1,0:T(8,128)S(1)} %get-tuple-element.239) | copy-start | bytes 6291460
  350.4 9.5 %all-to-all-start.1 = ((f32[1,8,512]{2,0,1:T(1,128)}), f32[1,8,512]{2,0,1:T(1,128)S(1)}, u32[]{:S(2)}, u32[]{:S(2)}) async-start(f32[1,8,512]{2,0,1:T(1,128)} %bitcast.1), calls=%async_computation.1 | async-start | bytes 32768 | tf_op jit(solution)/shard_map/all_to_all | solution.py:54
  358.0 7.3 %copy-start.2 = (u32[32]{0:T(128)S(1)}, u32[32]{0:T(128)}, u32[]{:S(2)}) copy-start(u32[32]{0:T(128)} %constant.132) | copy-start | bytes 388
  358.0 65.7 %copy-start.1 = (f32[16384]{0:T(1024)S(1)}, f32[16384]{0:T(1024)}, u32[]{:S(2)}) copy-start(f32[16384]{0:T(1024)} %get-tuple-element.448) | copy-start | bytes 196612
  359.9 65.7 %all-to-all-start.2 = ((f32[128,8,512]{2,0,1:T(8,128)}), f32[128,8,512]{2,0,1:T(8,128)S(1)}, u32[]{:S(2)}, u32[]{:S(2)}) async-start(f32[128,8,512]{2,0,1:T(8,128)} %copy.9), calls=%async_computation.2 | async-start | bytes 4194304 | tf_op jit(solution)/shard_map/all_to_all | solution.py:56
where the time goes:
time: 432 us; the launch traced here: 427 us
  other arithmetic  162 us (38%)
  local copies, waits for them, and re-layouts  121 us (28%)
  matrix products  74.2 us (17%)
  blocking collectives  56.4 us (13%)
  starting transfers between devices  11 us (3%)
    reduce_max x16, other arithmetic, top_step(): jnp.max(jnp.where(member, row_weights[:, None], floor_value), axis=0)  109 us
    gather x16, local copies, waits for them, and re-layouts, sum_step(): own_top = jnp.take(bin_top, row_bins)  92 us
    dot_general x16, matrix products, sum_step(): jnp.dot(row_states, spread, preferred_element_type=jnp.float32)  51.7 us
    unnamed x1, blocking collectives  48.1 us
    dot_general x16, matrix products, sum_step(): jnp.dot(ones_row, spread, preferred_element_type=jnp.float32)[0]  22.5 us
    max x16, other arithmetic, top_step(): jnp.maximum(carry, jnp.max(jnp.where(member, row_weights[:, None], floor_...  20.7 us
    convert_element_type x16, other arithmetic, sum_step(): scaled = jnp.exp(row_weights - own_top).astype(jnp.bfloat16)  11.2 us
    gather x16, other arithmetic, sum_step(): own_top = jnp.take(bin_top, row_bins)  11.1 us
  transfers between devices with their start and end apart: 2, of which 0 were waited for; matrix products, arithmetic and copies ran while one was open for 4% of the time, Pallas kernels for 0%

commit v1 on v0

v1 whole, which is shorter than its diff:
```python
import functools

import jax
import jax.numpy as jnp
from jax import lax
from jax.experimental import pallas as pl
from jax.experimental.pallas import tpu as pltpu
from jax.sharding import PartitionSpec as P

BINS = 4096
LANES = 128
QUARTERS = 4
SPAN = BINS // QUARTERS
PIECE = 256

floor_value = -10000.0
far = -1.0e30


def local_kernel(groups, lw_ref, bins_ref, st_ref, out_ref, peak_ref, top_ref, w_ref, rest_ref, quarter_ref,
                 left0, right0, left1, right1, acc_ref):
    rows = lw_ref.shape[0]
    states = st_ref.shape[0]
    highs = BINS // LANES
    subs = LANES // 8
    peak_ref[...] = jnp.full(peak_ref.shape, far, jnp.float32)
    label = lax.broadcasted_iota(jnp.int32, (subs, 8, LANES), 0) * 8 + lax.broadcasted_iota(jnp.int32, (subs, 8, LANES), 1)

    def peak_step(index, carry):
        weights, highs_of, gates = [], [], []
        for half in range(2):
            row = index * 2 + half
            weights.append(jnp.broadcast_to(lw_ref[pl.ds(row, 1), :], (8, LANES)))
            row_bins = jnp.broadcast_to(bins_ref[pl.ds(row, 1), :], (8, LANES))
            highs_of.append(row_bins >> 7)
            gates.append(jnp.where(label == (row_bins & 127)[None], jnp.float32(0.0), jnp.float32(far)))
        for high in range(highs):
            parts = [gates[half] + jnp.where(highs_of[half] == high, weights[half], far)[None] for half in range(2)]
            peak_ref[high] = jnp.maximum(peak_ref[high], jnp.maximum(parts[0], parts[1]))
        return carry

    lax.fori_loop(0, rows // 2, peak_step, 0)
    for high in range(highs):
        table = peak_ref[high].reshape(LANES, LANES)
        top_ref[high:high + 1, :] = jnp.maximum(jnp.max(table.T, axis=0, keepdims=True), floor_value)

    own_bins = bins_ref[...]
    low = own_bins & 127
    high_of = own_bins >> 7
    own = jnp.zeros((rows, LANES), jnp.float32)
    for high in range(highs):
        line = jnp.broadcast_to(top_ref[high:high + 1, :], (rows, LANES))
        own = jnp.where(high_of == high, jnp.take_along_axis(line, low, axis=1, mode="promise_in_bounds"), own)
    w_ref[...] = jnp.exp(lw_ref[...] - own).astype(jnp.bfloat16).astype(jnp.float32)
    rest_ref[...] = (own_bins & (SPAN - 1)).astype(jnp.float32)
    quarter_ref[...] = (own_bins >> 10).astype(jnp.float32)

    acc_ref[...] = jnp.zeros(acc_ref.shape, jnp.float32)
    block_rows = left0.shape[1] // LANES
    blocks = rows // block_rows
    tall = PIECE // 16
    count16 = lax.broadcasted_iota(jnp.int32, (tall, 16, LANES), 0) * 16 + lax.broadcasted_iota(jnp.int32, (tall, 16, LANES), 1)
    count16 = count16.astype(jnp.float32).astype(jnp.bfloat16)
    line16 = lax.broadcasted_iota(jnp.int32, (16, LANES), 0).astype(jnp.float32).astype(jnp.bfloat16)
    zero = jnp.zeros((), jnp.bfloat16)

    def build(block, left, right):
        for step in range(block_rows):
            row = block * block_rows + step
            cols = slice(step * LANES, (step + 1) * LANES)
            weight = jnp.broadcast_to(w_ref[pl.ds(row, 1), :], (16, LANES)).astype(jnp.bfloat16)
            rest = jnp.broadcast_to(rest_ref[pl.ds(row, 1), :], (16, LANES))
            quarter = jnp.broadcast_to(quarter_ref[pl.ds(row, 1), :], (16, LANES)).astype(jnp.bfloat16)
            for piece in range(SPAN // PIECE):
                shifted = (rest - float(piece * PIECE)).astype(jnp.bfloat16)
                spread = jnp.where(count16 == shifted[None], weight[None], zero)
                right[piece * PIECE:(piece + 1) * PIECE, cols] = spread.reshape(PIECE, LANES)
            state = st_ref[:, pl.ds(pl.multiple_of(row * LANES, LANES), LANES)].reshape(states // 16, 16, LANES)
            for part in range(QUARTERS):
                kept = jnp.where((quarter == jnp.bfloat16(part))[None], state, zero)
                left[part * states:(part + 1) * states, cols] = kept.reshape(states, LANES)
            left[QUARTERS * states:, cols] = jnp.where(line16 == quarter, jnp.ones((), jnp.bfloat16), zero)

    def gather_in(left, right):
        acc_ref[...] += lax.dot_general(left[...], right[...], (((1,), (1,)), ((), ())), preferred_element_type=jnp.float32)

    build(0, left0, right0)

    def pair_step(index, carry):
        build(index * 2 + 1, left1, right1)
        gather_in(left0, right0)
        build(jnp.minimum(index * 2 + 2, blocks - 1), left0, right0)
        gather_in(left1, right1)
        return carry

    lax.fori_loop(0, blocks // 2, pair_step, 0)

    owned = BINS // groups
    device_top = jnp.max(jnp.max(top_ref[...], axis=1, keepdims=True), axis=0, keepdims=True)
    lane = lax.broadcasted_iota(jnp.int32, (1, LANES), 1)
    masses = jnp.zeros((1, LANES), jnp.float32)
    for group in range(groups):
        first = group * owned
        part, offset = first // SPAN, first % SPAN
        out_ref[group, 0:states, :] = acc_ref[part * states:(part + 1) * states, offset:offset + owned]
        mass = acc_ref[QUARTERS * states + part:QUARTERS * states + part + 1, offset:offset + owned]
        out_ref[group, states:states + 1, :] = mass
        subtotal = jnp.zeros((1, LANES), jnp.float32)
        for tile in range(owned // LANES):
            span = slice(tile * LANES, (tile + 1) * LANES)
            line = top_ref[first // LANES + tile:first // LANES + tile + 1, :]
            out_ref[group, states + 1:states + 2, span] = line
            subtotal = subtotal + mass[:, span] * jnp.exp(line - device_top)
        masses = jnp.where(lane == group, jnp.sum(subtotal, axis=1, keepdims=True), masses)
    for group in range(groups):
        out_ref[group, states + 2:states + 8, :] = jnp.zeros((6, owned), jnp.float32)
        out_ref[group, states + 2:states + 3, 0:LANES] = masses
        out_ref[group, states + 3:states + 4, 0:LANES] = jnp.broadcast_to(device_top, (1, LANES))


def local_pairs(log_weights, bins, states, groups):
    count = log_weights.shape[0]
    rows = count // LANES
    width = states.shape[0]
    block = min(1024, count // 2)
    owned = BINS // groups
    tall = QUARTERS * width + 16
    return pl.pallas_call(
        functools.partial(local_kernel, groups),
        out_shape=jax.ShapeDtypeStruct((groups, width + 8, owned), jnp.float32),
        in_specs=[pl.BlockSpec(memory_space=pltpu.VMEM)] * 3,
        out_specs=pl.BlockSpec(memory_space=pltpu.VMEM),
        scratch_shapes=[
            pltpu.VMEM((BINS // LANES, LANES // 8, 8, LANES), jnp.float32),
            pltpu.VMEM((BINS // LANES, LANES), jnp.float32),
            pltpu.VMEM((rows, LANES), jnp.float32),
            pltpu.VMEM((rows, LANES), jnp.float32),
            pltpu.VMEM((rows, LANES), jnp.float32),
            pltpu.VMEM((tall, block), jnp.bfloat16),
            pltpu.VMEM((SPAN, block), jnp.bfloat16),
            pltpu.VMEM((tall, block), jnp.bfloat16),
            pltpu.VMEM((SPAN, block), jnp.bfloat16),
            pltpu.VMEM((tall, SPAN), jnp.float32),
        ],
        name="local_pairs",
    )(log_weights.reshape(rows, LANES), bins.reshape(rows, LANES), states)


def body(log_weights, bins, states):
    groups = lax.axis_size("dom")
    width = states.shape[0]
    packed = local_pairs(log_weights, bins, states, groups)
    packed = lax.all_to_all(packed, "dom", split_axis=0, concat_axis=0, tiled=True)
    top_pieces = packed[:, width + 1, :]
    owned_top = jnp.max(top_pieces, axis=0)
    factor = jnp.exp(top_pieces - owned_top[None, :])
    owned_mass = jnp.sum(packed[:, width, :] * factor, axis=0)
    owned_sums = jnp.sum(packed[:, :width, :] * factor[:, None, :], axis=0)
    bin_means = owned_sums / jnp.maximum(owned_mass, 1.0)[None, :]
    group_masses = packed[:, width + 2, :groups]
    group_tops = packed[:, width + 3, 0]
    top = jnp.max(group_tops)
    scaled_masses = jnp.sum(group_masses * jnp.exp(group_tops - top)[:, None], axis=0)
    total = jnp.sum(scaled_masses)
    lower = lax.iota(jnp.int32, groups) < lax.axis_index("dom")
    before = jnp.sum(jnp.where(lower, scaled_masses, jnp.float32(0.0)))
    share = owned_mass * jnp.exp(owned_top - top)
    cumulative = (before + jnp.cumsum(share)) / total
    whole_count = log_weights.shape[0] * groups
    particle_weights = whole_count * jnp.exp(log_weights - top) / total
    return (cumulative, bin_means, particle_weights)


def solution(mesh):
    placed = (P(("filt", "dom")), P(("filt", "dom")), P(None, ("filt", "dom")))
    return jax.shard_map(
        body,
        mesh=mesh,
        in_specs=placed,
        out_specs=(P(("filt", "dom")), P(None, ("filt", "dom")), P(("filt", "dom"))),
        check_vma=False,
    )
```

time: 432 us -> 116 us (0.27)
  the two profiles are of different devices: /device:TPU:16 before, /device:TPU:0 now
where the time goes in v1:
time: 116 us
  waiting for transfers between devices  51.8 us (45%)
  Pallas kernels  47.7 us (41%)
  other arithmetic  8.73 us (8%)
  starting transfers between devices  6.47 us (6%)
    all_to_all x1, waiting for transfers between devices, body(): lax.all_to_all(packed, 'dom', split_axis=0, concat_axis=0, tiled=True)  51.8 us
    pallas_call x1, Pallas kernels, local_pairs(): pl.pallas_call(functools.partial(local_kernel, groups), out_shape=jax.Sha...  47.7 us
    all_to_all x1, starting transfers between devices, body(): lax.all_to_all(packed, 'dom', split_axis=0, concat_axis=0, tiled=True)  6.47 us
  transfers between devices with their start and end apart: 1, of which 1 were waited for; matrix products, arithmetic and copies ran while one was open for 0% of the time, Pallas kernels for 0%

profile of v1, /device:TPU:0, one launch (start us, length us, event | category | flops | bytes accessed | tf_op | source)
XLA Modules:
  0.0 115.6 jit_solution(5716930640202662972)
XLA Ops:
  0.6 47.7 %local_pairs.1 = f32[8,136,512]{2,1,0:T(8,128)} custom-call(f32[128,128]{1,0:T(8,128)} %bitcast.22, s32[128,128]{1,0:T(8,128)} %bitcast.23, bf16[128,16384]{1,0:T(8,128)(2,1)} %st_ref.1), custom_call_target="tpu_custom_call" | custom-call | tf_op jit(solution)/shard_map/local_pairs/pallas_call | solution.py:128
  48.3 0.0 copy-start
  48.3 6.5 %all-to-all-start = ((f32[8,136,512]{2,1,0:T(8,128)}), f32[8,136,512]{2,1,0:T(8,128)S(1)}, u32[]{:S(2)}, u32[]{:S(2)}) async-start(f32[8,136,512]{2,1,0:T(8,128)} %local_pairs.1), calls=%async_computation | async-start | bytes 4456448 | tf_op jit(solution)/shard_map/all_to_all | solution.py:153
  54.8 51.8 %all-to-all-done = f32[8,136,512]{2,1,0:T(8,128)S(1)} async-done(((f32[8,136,512]{2,1,0:T(8,128)}), f32[8,136,512]{2,1,0:T(8,128)S(1)}, u32[]{:S(2)}, u32[]{:S(2)}) %all-to-all-start) | async-done | bytes 2228256 | tf_op jit(solution)/shard_map/all_to_all | solution.py:153
  106.8 0.6 slice_reduce_fusion
  107.4 0.7 broadcast_maximum_fusion
  108.0 0.3 reduce-window.9
  108.4 0.1 slice.26
  108.5 0.1 slice_reduce_fusion.1
  108.6 0.8 exponential_reduce_fusion
  109.4 0.8 multiply_reduce_fusion.1
  110.1 0.0 copy-done
  110.1 2.0 %multiply_divide_fusion = f32[16384]{0:T(1024)} fusion(f32[16384]{0:T(1024)S(1)} %copy-done, f32[]{:T(128)} %get-tuple-element.4, f32[]{:T(128)} %slice_reduce_fusion), kind=kLoop, calls=%fused_computation.3 | loop fusion | flops 49152 | bytes 131080 | tf_op jit(solution)/shard_map/div | solution.py:170
  112.1 0.3 fusion
  112.4 0.7 broadcast_divide_fusion
  113.1 0.6 fusion.4
  113.7 1.9 %divide_bitcast_fusion = f32[512]{0:T(512)} fusion(f32[4,128]{1,0:T(4,128)S(1)} %reduce-window.9, f32[]{:T(128)} %get-tuple-element.4, f32[4]{0:T(128)S(1)} %slice_reduce_fusion.1, f32[]{:T(128)} %fusion.4), kind=kLoop, calls=%fused_computation.15 | loop fusion | flops 1536 | bytes 4120 | tf_op jit(solution)/shard_map/div | solution.py:168
  (6 shorter events, 0.1 us)
Async XLA Ops:
  48.3 61.8 %copy-start = (f32[16384]{0:T(1024)S(1)}, f32[16384]{0:T(1024)}, u32[]{:S(2)}) copy-start(f32[16384]{0:T(1024)} %param.3) | copy-start | bytes 196612
  48.3 58.3 %all-to-all-start = ((f32[8,136,512]{2,1,0:T(8,128)}), f32[8,136,512]{2,1,0:T(8,128)S(1)}, u32[]{:S(2)}, u32[]{:S(2)}) async-start(f32[8,136,512]{2,1,0:T(8,128)} %local_pairs.1), calls=%async_computation | async-start | bytes 4456448 | tf_op jit(solution)/shard_map/all_to_all | solution.py:153
